TPU v7x, 16 devices: a 4x2x1 block of a 4x4x8 slice. The times are simulated.
16 devices in a mesh: dp: 2 (over y, z), tp: 8 (over x, core).
Axes of the slice: x: 4, y: 2, z: 1, core: 2. Of those that a mesh axis runs over, the one named last changes fastest.
The devices are a block of a 4x4x8 slice.
Arguments:
- queries: bfloat16 [256, 256], P(('dp', 'tp')), parts along dimension 0
- w_first: bfloat16 [256, 1024], replicated
- w_second: bfloat16 [1024, 256], replicated
- catalogue: bfloat16 [262144, 256], P('tp')
- log_q: float32 [262144], P('tp')
- labels: int32 [256], P(('dp', 'tp')), parts along dimension 0
Outputs:
- output 1: float32 [2], P('dp'), parts along dimension 0
- output 2: bfloat16 [524288, 256], P(('dp', 'tp')), parts along dimension 0
- output 3: bfloat16 [512, 1024], P('dp'), parts along dimension 0
- output 4: bfloat16 [2048, 256], P('dp'), parts along dimension 0
There are 2 independent parts. A program takes and returns all parts, laid end to end along the dimension named above; an argument that names none is the same for every part.
All inputs are finite; a program needn't handle non-finite values.
Results may differ from a plain program's by a relative error of at most 0.00349722.
Values are sent between devices in bfloat16 or wider.
A program may use at most 768 MiB of HBM per device.

v0:
```python
import jax
import jax.numpy as jnp
from jax import lax
from jax.sharding import PartitionSpec as P


def solution(mesh):
    def local_step(queries, w_first, w_second, catalogue, log_q, labels):
        items_local = catalogue.shape[0]
        shard_index = lax.axis_index("tp")
        pre_act = jnp.dot(queries, w_first, preferred_element_type=jnp.float32)
        hidden = jnp.maximum(pre_act, 0.0).astype(jnp.bfloat16)
        query_emb = jnp.dot(hidden, w_second, preferred_element_type=jnp.float32).astype(jnp.bfloat16)
        emb_all = lax.all_gather(query_emb, "tp", axis=0, tiled=True)
        labels_all = lax.all_gather(labels, "tp", axis=0, tiled=True)
        total_rows = emb_all.shape[0]
        logits = lax.dot_general(emb_all, catalogue, (((1,), (1,)), ((), ())), preferred_element_type=jnp.float32) - log_q[None, :]
        local_max = jnp.max(logits, axis=1)
        local_ids = labels_all - shard_index * items_local
        label_hit = lax.broadcasted_iota(jnp.int32, (1, items_local), 1) == local_ids[:, None]
        local_target = jnp.sum(jnp.where(label_hit, logits, 0.0), axis=1)
        exp_local = jnp.exp(logits - local_max[:, None])
        local_sum = jnp.sum(exp_local, axis=1)
        row_max = lax.pmax(local_max, "tp")
        rescale = jnp.exp(local_max - row_max)
        row_stats = lax.psum(jnp.stack([local_sum * rescale, local_target]), "tp")
        sum_exp = row_stats[0]
        mean_loss = jnp.mean(row_max + jnp.log(sum_exp) - row_stats[1]).reshape(1)
        soft_prob = exp_local * (rescale / sum_exp)[:, None]
        grad_logits = (jnp.where(label_hit, soft_prob - 1.0, soft_prob) / total_rows).astype(jnp.bfloat16)
        grad_items = lax.dot_general(grad_logits, emb_all, (((0,), (0,)), ((), ())), preferred_element_type=jnp.float32).astype(jnp.bfloat16)
        emb_part = jnp.dot(grad_logits, catalogue, preferred_element_type=jnp.float32)
        grad_emb = lax.psum_scatter(emb_part, "tp", scatter_dimension=0, tiled=True).astype(jnp.bfloat16)
        second_part = lax.dot_general(hidden, grad_emb, (((0,), (0,)), ((), ())), preferred_element_type=jnp.float32)
        grad_hidden = lax.dot_general(grad_emb, w_second, (((1,), (1,)), ((), ())), preferred_element_type=jnp.float32)
        grad_pre = jnp.where(pre_act > 0.0, grad_hidden, 0.0).astype(jnp.bfloat16)
        first_part = lax.dot_general(queries, grad_pre, (((0,), (0,)), ((), ())), preferred_element_type=jnp.float32)
        grad_first, grad_second = lax.psum((first_part, second_part), "tp")
        return mean_loss, grad_items, grad_first.astype(jnp.bfloat16), grad_second.astype(jnp.bfloat16)

    row_spec = P(("dp", "tp"), None)
    return jax.shard_map(local_step, mesh=mesh, in_specs=(row_spec, P(None, None), P(None, None), P("tp", None), P("tp"), P(("dp", "tp"))), out_specs=(P("dp"), row_spec, P("dp", None), P("dp", None)), check_vma=False)
```

profile of v0, /device:TPU:113, one launch (start us, length us, event | category | flops | bytes accessed | tf_op | source)
XLA Modules:
  0.0 200.4 jit_solution(2400465087520876393)
XLA Ops:
  7.2 0.0 copy-start
  7.2 0.1 reduce-scatter.2.cloned.1.call-start
  7.3 1.3 fusion.16
  8.6 0.2 convolution_convert_fusion.1
  8.7 19.0 %all_gather.6 = bf16[128,256]{1,0:T(8,128)(2,1)S(1)} all-gather(bf16[16,256]{1,0:T(8,128)(2,1)S(1)} %convolution_convert_fusion.1), channel_id=1, replica_groups=mesh['dp'=2,'tp'=8] {'tp'}, dimensions={0}, use_global_device_ids=true | all-gather | bytes 73728 | tf_op jit(solution)/shard_map/all_gather | solution.py:14
  27.7 1.2 dynamic-slice
  29.6 0.9 dynamic-update-slice
  30.5 11.1 %all-reduce = s32[128]{0:T(128)S(1)} all-reduce(s32[128]{0:T(128)S(1)} %dynamic-update-slice), channel_id=1, replica_groups=mesh['dp'=2,'tp'=8] {'tp'}, use_global_device_ids=true, to_apply=%add | all-reduce | flops 128 | bytes 1024
  41.6 12.7 %fusion.15 = (f32[128]{0:T(128)S(1)}, f32[128,32768]{1,0:T(8,128)}) fusion(f32[32768]{0:T(1024)} %param.10, bf16[128,256]{1,0:T(8,128)(2,1)S(1)} %all_gather.6, bf16[32768,256]{1,0:T(8,128)(2,1)} %param.9), kind=kOutput, calls=%fused_computation.31 | convolution fusion | flops 2155872256 | bytes 33751552 | tf_op jit(solution)/shard_map/dot_general | solution.py:17
  54.3 14.1 %pmax.7 = f32[128]{0:T(128)S(1)} all-reduce(f32[128]{0:T(128)S(1)} %get-tuple-element.14), channel_id=1, replica_groups=mesh['dp'=2,'tp'=8] {'tp'}, use_global_device_ids=true, to_apply=%region_1.2 | all-reduce | flops 128 | bytes 1024 | tf_op jit(solution)/shard_map/pmax | solution.py:24
  68.4 8.4 %fusion.2 = (f32[128]{0:T(128)S(1)}, f32[128]{0:T(128)S(1)}) fusion(f32[128,32768]{1,0:T(8,128)} %get-tuple-element.15, f32[128]{0:T(128)S(1)} %get-tuple-element.14, s32[128]{0:T(128)S(1)} %broadcast_subtract_fusion), kind=kLoop, calls=%fused_computation.8 | loop fusion | flops 20971264 | bytes 16779264 | tf_op jit(solution)/shard_map/reduce_sum | solution.py:23
  76.8 12.9 %psum.21 = f32[2,128]{1,0:T(2,128)S(1)} all-reduce(f32[2,128]{1,0:T(2,128)S(1)} %pad_maximum_fusion), channel_id=1, replica_groups=mesh['dp'=2,'tp'=8] {'tp'}, use_global_device_ids=true, to_apply=%region_4.5 | all-reduce | flops 256 | bytes 2048 | tf_op jit(solution)/shard_map/psum | solution.py:26
  89.7 0.6 bitcast_divide_fusion
  90.3 8.4 %fusion.1 = bf16[128,32768]{1,0:T(8,128)(2,1)S(1)} fusion(f32[128,32768]{1,0:T(8,128)} %get-tuple-element.15, f32[128]{0:T(128)S(1)} %get-tuple-element.12, s32[128]{0:T(128)S(1)} %broadcast_subtract_fusion, f32[128]{0:T(128)S(1)} %get-tuple-element.14), kind=kLoop, calls=%fused_computation.4 | loop fusion | flops 29360128 | bytes 25167360 | tf_op jit(solution)/shard_map/convert_element_type | solution.py:30
  98.7 3.2 %copy-done.1 = bf16[128,32768]{1,0:T(8,128)(2,1)} copy-done((bf16[128,32768]{1,0:T(8,128)(2,1)}, bf16[128,32768]{1,0:T(8,128)(2,1)S(1)}, u32[]{:S(2)}) %copy-start.1) | copy-done | bytes 8388632
  101.9 8.8 %fusion.17 = f32[128,256]{1,0:T(8,128)} fusion(bf16[128,32768]{1,0:T(8,128)(2,1)S(1)} %fusion.1, bf16[32768,256]{1,0:T(8,128)(2,1)} %param.9), kind=kOutput, calls=%fused_computation.33 | convolution fusion | flops 2147483648 | bytes 25296896 | tf_op jit(solution)/shard_map/dot_general | solution.py:32
  110.7 0.1 reduce-scatter.2.cloned.1.call-update
  110.8 0.0 copy-start.2
  110.8 14.1 %convolution_convert_fusion = bf16[32768,256]{1,0:T(8,128)(2,1)} fusion(bf16[128,32768]{1,0:T(8,128)(2,1)} %copy-done.1, bf16[128,256]{1,0:T(8,128)(2,1)S(1)} %all_gather.6), kind=kOutput, calls=%fused_computation | convolution fusion | flops 2155872256 | bytes 25231360 | tf_op jit(solution)/shard_map/dot_general | solution.py:31
  125.5 8.6 %reduce-scatter.2.cloned.1.call-done = f32[16,256]{1,0:T(8,128)} async-done(((f32[128,256]{1,0:T(8,128)}), f32[16,256]{1,0:T(8,128)}) %reduce-scatter.2.cloned.1.call-update) | async-done | bytes 16400 | tf_op jit(solution)/shard_map/reduce_scatter | solution.py:33
  134.2 1.3 convolution_bitcast_fusion
  135.4 1.0 fusion.6
  136.5 55.0 %all-reduce.3 = (bf16[256,1024]{0,1:T(8,128)(2,1)S(1)}, bf16[1024,256]{1,0:T(8,128)(2,1)}) all-reduce(f32[256,1024]{0,1:T(8,128)S(1)} %convolution_bitcast_fusion, f32[1024,256]{1,0:T(8,128)S(1)} %fusion.6), channel_id=1, replica_groups=mesh['dp'=2,'tp'=8] {'tp'}, use_global_device_ids=true, to_apply=%region_7.8 | all-reduce | flops 524288 | bytes 3145728 | tf_op jit(solution)/shard_map/psum | solution.py:38
  191.4 1.0 copy.10
  (7 shorter events, 0.0 us)
Async XLA Ops:
  7.2 1.4 copy-start
  7.2 127.0 %reduce-scatter.2.cloned.1.call-start = ((), (), s32[]{:S(2)}) async-start(), calls=%async_computation.1 | async-start | bytes 147456 | tf_op jit(solution)/shard_map/reduce_scatter | solution.py:33
  98.7 3.2 %copy-start.1 = (bf16[128,32768]{1,0:T(8,128)(2,1)}, bf16[128,32768]{1,0:T(8,128)(2,1)S(1)}, u32[]{:S(2)}) copy-start(bf16[128,32768]{1,0:T(8,128)(2,1)S(1)} %fusion.1) | copy-start | bytes 25165828
  110.8 23.4 %copy-start.2 = (bf16[16,256]{1,0:T(8,128)(2,1)S(1)}, bf16[16,256]{1,0:T(8,128)(2,1)}, u32[]{:S(2)}) copy-start(bf16[16,256]{1,0:T(8,128)(2,1)} %param.6) | copy-start | bytes 24580
Sparse Core Ops, SparseCore 0:
  110.9 23.2 reduce-scatter.1
where the time goes:
time: 202 us; the launch traced here: 200 us
  blocking collectives  112 us (55%)
  matrix products  39.3 us (19%)
  other arithmetic  17.4 us (9%)
  between operations  16.6 us (8%)
  waiting for transfers between devices  8.68 us (4%)
  local copies, waits for them, and re-layouts  6.33 us (3%)
    psum x1, blocking collectives, local_step(): grad_first, grad_second = lax.psum((first_part, second_part), 'tp')  55 us
    all_gather x1, blocking collectives, local_step(): emb_all = lax.all_gather(query_emb, 'tp', axis=0, tiled=True)  19 us
    dot_general x1, matrix products, local_step(): lax.dot_general(grad_logits, emb_all, (((0,), (0,)), ((), ())), preferred...  14.1 us
    pmax x1, blocking collectives, local_step(): row_max = lax.pmax(local_max, 'tp')  14.1 us
    psum x1, blocking collectives, local_step(): row_stats = lax.psum(jnp.stack([local_sum * rescale, local_target]), 'tp')  12.9 us
    dot_general x1, matrix products, local_step(): lax.dot_general(emb_all, catalogue, (((1,), (1,)), ((), ())), preferred_e...  12.7 us
    unnamed x1, blocking collectives  11.1 us
    dot_general x1, matrix products, local_step(): jnp.dot(grad_logits, catalogue, preferred_element_type=jnp.float32)  8.76 us
  transfers between devices with their start and end apart: 1, of which 1 were waited for; matrix products, arithmetic and copies ran while one was open for 7% of the time, Pallas kernels for 0%

commit v1 on v0

v1 whole, which is shorter than its diff:
```python
import functools

import jax
import jax.numpy as jnp
from jax import lax
from jax.experimental import pallas as pl
from jax.experimental.pallas import tpu as pltpu
from jax.sharding import PartitionSpec as P

F32, BF16 = jnp.float32, jnp.bfloat16
MESH = pl.DeviceIdType.MESH
LANES = 128
FIRST_TILE = 4096
SECOND_TILE = 4096
LOAD_TILE = 2048
OUT_TILE = 2048
OUT_SLOTS = 4
LOWEST = -3.0e38


def dot(a, b, contract):
    return lax.dot_general(a, b, ((contract[:1], contract[1:]), ((), ())), preferred_element_type=F32)


def loss_kernel(n, q_hbm, w1_hbm, w2_hbm, cat_hbm, lq_hbm, labels,
                g_ref, x_ref, dx_ref, h_ref, a_ref, q_ref, w2_ref, loss_ref,
                cat, ez, lq, w1, lab, d, m_run, s_run, t_run, m_hist, stats, part, pieces,
                load_sem, cat_sem, send_sem, q_sem, lab_sem, stat_sem, part_sem, dx_sem):
    me = lax.axis_index("tp")
    own = q_hbm.shape[0]
    rows = own * n
    items = cat_hbm.shape[0]
    my_rows = pl.ds(pl.multiple_of(me * own, own), own)

    q_load = pltpu.make_async_copy(q_hbm, q_ref.at[my_rows], load_sem.at[0])
    w1_load = pltpu.make_async_copy(w1_hbm, w1, load_sem.at[1])
    w2_load = pltpu.make_async_copy(w2_hbm, w2_ref, load_sem.at[2])
    lq_load = pltpu.make_async_copy(lq_hbm, lq, load_sem.at[3])
    q_load.start()
    barrier = pltpu.get_barrier_semaphore()
    peers = [lax.rem(me + k, n) for k in range(1, n)]
    for p in peers:
        pl.semaphore_signal(barrier, inc=1, device_id={"tp": p}, device_id_type=MESH)
    w1_load.start()
    w2_load.start()
    lq_load.start()
    for j in range(items // LOAD_TILE):
        part_rows = pl.ds(j * LOAD_TILE, LOAD_TILE)
        pltpu.make_async_copy(cat_hbm.at[part_rows], cat.at[part_rows], cat_sem.at[j]).start()
    for r in range(own):
        lab[pl.ds(me * own + r, 1), :] = jnp.full((1, LANES), labels[r], jnp.int32)
    pl.semaphore_wait(barrier, n - 1)

    def exchange(src, dst, stage, recv_sem):
        copies = []
        for k, p in enumerate(peers):
            copy = pltpu.make_async_remote_copy(
                src_ref=src(p), dst_ref=dst, send_sem=send_sem.at[stage, k], recv_sem=recv_sem.at[me],
                device_id={"tp": p}, device_id_type=MESH)
            copy.start()
            copies.append(copy)
        return copies

    def arrive(dst_of, recv_sem):
        for p in peers:
            ref = dst_of(p)
            pltpu.make_async_copy(ref, ref, recv_sem.at[p]).wait()

    def rows_of(p):
        return pl.ds(pl.multiple_of(p * own, own), own)

    lab_sends = exchange(lambda p: lab.at[my_rows], lab.at[my_rows], 0, lab_sem)
    q_load.wait()
    q_sends = exchange(lambda p: q_ref.at[my_rows], q_ref.at[my_rows], 1, q_sem)
    m_run[...] = jnp.full(m_run.shape, LOWEST, F32)
    s_run[...] = jnp.zeros(s_run.shape, F32)
    t_run[...] = jnp.zeros(t_run.shape, F32)
    w1_load.wait()
    w2_load.wait()
    lq_load.wait()
    arrive(lambda p: lab.at[rows_of(p)], lab_sem)
    d[...] = lab[...] - me * items - lax.broadcasted_iota(jnp.int32, d.shape, 1)
    arrive(lambda p: q_ref.at[rows_of(p)], q_sem)

    a = dot(q_ref[...], w1[...], (1, 0))
    a_ref[...] = a
    h_ref[...] = jnp.maximum(a, 0.0).astype(BF16)
    x_ref[...] = dot(h_ref[...], w2_ref[...], (1, 0)).astype(BF16)

    def first_pass(i, carry):
        for j in range(FIRST_TILE // LOAD_TILE):
            k = i * (FIRST_TILE // LOAD_TILE) + j
            part_rows = pl.ds(pl.multiple_of(k * LOAD_TILE, LOAD_TILE), LOAD_TILE)
            pltpu.make_async_copy(cat_hbm.at[part_rows], cat.at[part_rows], cat_sem.at[k]).wait()
        base = pl.multiple_of(i * FIRST_TILE, FIRST_TILE)
        z = dot(x_ref[...], cat[pl.ds(base, FIRST_TILE), :], (1, 1)) - lq[:, pl.ds(base, FIRST_TILE)]
        m_old = m_run[...]
        m = m_old
        for c in range(FIRST_TILE // LANES):
            m = jnp.maximum(m, z[:, c * LANES:(c + 1) * LANES])
        s = s_run[...] * jnp.exp(m_old - m)
        t = t_run[...]
        dd = d[...]
        for c in range(FIRST_TILE // LANES):
            zc = z[:, c * LANES:(c + 1) * LANES]
            e = jnp.exp(zc - m)
            s = s + e
            t = jnp.where(dd == base + c * LANES, zc, t)
            ez[:, pl.ds(pl.multiple_of(base + c * LANES, LANES), LANES)] = e
        m_run[...] = m
        m_hist[i] = m
        s_run[...] = s
        t_run[...] = t
        return carry

    lax.fori_loop(0, items // FIRST_TILE, first_pass, 0)

    m_t = m_run[...].T
    m_row = jnp.max(m_t, axis=0, keepdims=True)
    s_row = jnp.sum(s_run[...].T * jnp.exp(m_t - m_row), axis=0, keepdims=True)
    t_row = jnp.sum(t_run[...].T, axis=0, keepdims=True)
    sub = lax.broadcasted_iota(jnp.int32, (8, LANES), 0)
    stats[me] = jnp.where(sub == 0, m_row, jnp.where(sub == 1, s_row, t_row))
    stat_sends = exchange(lambda p: stats.at[me], stats.at[me], 2, stat_sem)
    arrive(lambda p: stats.at[p], stat_sem)
    big = stats[0, 0:1, :]
    for p in range(1, n):
        big = jnp.maximum(big, stats[p, 0:1, :])
    total = jnp.zeros_like(big)
    target = jnp.zeros_like(big)
    for p in range(n):
        total = total + stats[p, 1:2, :] * jnp.exp(stats[p, 0:1, :] - big)
        target = target + stats[p, 2:3, :]
    loss_ref[...] = jnp.sum(big + jnp.log(total) - target, axis=1, keepdims=True) / rows
    big_col = jnp.broadcast_to(big, (rows, LANES)).T
    inv_col = jnp.broadcast_to(1.0 / (total * rows), (rows, LANES)).T

    part[...] = jnp.zeros(part.shape, F32)

    def second_pass(i, carry):
        base = pl.multiple_of(i * SECOND_TILE, SECOND_TILE)
        dd = d[...]
        for f in range(SECOND_TILE // FIRST_TILE):
            scale = jnp.exp(m_hist[i * (SECOND_TILE // FIRST_TILE) + f] - big_col) * inv_col
            for c in range(f * FIRST_TILE // LANES, (f + 1) * FIRST_TILE // LANES):
                cols = pl.ds(pl.multiple_of(base + c * LANES, LANES), LANES)
                g = ez[:, cols] * scale
                g = g - jnp.where(dd == base + c * LANES, 1.0 / rows, 0.0)
                g_ref[:, cols] = g.astype(BF16)
        part[...] += dot(g_ref[:, pl.ds(base, SECOND_TILE)], cat[pl.ds(base, SECOND_TILE), :], (1, 0))
        return carry

    lax.fori_loop(0, items // SECOND_TILE, second_pass, 0)

    part_sends = exchange(lambda p: part.at[rows_of(p)], pieces.at[me], 3, part_sem)
    pieces[me] = part[my_rows, :]
    arrive(lambda p: pieces.at[p], part_sem)
    acc = pieces[0]
    for p in range(1, n):
        acc = acc + pieces[p]
    dx_ref[my_rows, :] = acc.astype(BF16)
    dx_sends = exchange(lambda p: dx_ref.at[my_rows], dx_ref.at[my_rows], 4, dx_sem)
    arrive(lambda p: dx_ref.at[rows_of(p)], dx_sem)
    for copy in lab_sends + q_sends + stat_sends + part_sends + dx_sends:
        copy.wait_send()


def grad_kernel(g_ref, x_ref, dx_ref, h_ref, a_ref, q_ref, w2_ref, loss_ref,
                loss_hbm, de_hbm, dw1_hbm, dw2_hbm, stage, dw1, dw2, out_sem, sem):
    items = de_hbm.shape[0]
    steps = items // OUT_TILE
    pltpu.make_async_copy(loss_ref, loss_hbm, sem.at[0]).start()

    def out_copy(i, slot):
        at = pl.ds(pl.multiple_of(i * OUT_TILE, OUT_TILE), OUT_TILE)
        return pltpu.make_async_copy(stage.at[slot], de_hbm.at[at], out_sem.at[slot])

    def step(i, carry):
        slot = lax.rem(i, OUT_SLOTS)

        @pl.when(i >= OUT_SLOTS)
        def _():
            out_copy(i - OUT_SLOTS, slot).wait()

        base = pl.multiple_of(i * OUT_TILE, OUT_TILE)
        stage[slot] = dot(g_ref[:, pl.ds(base, OUT_TILE)], x_ref[...], (0, 0)).astype(BF16)
        out_copy(i, slot).start()
        return carry

    lax.fori_loop(0, OUT_SLOTS, step, 0)
    dx = dx_ref[...]
    dw2[...] = dot(h_ref[...], dx, (0, 0)).astype(BF16)
    pltpu.make_async_copy(dw2, dw2_hbm, sem.at[2]).start()
    dh = dot(dx, w2_ref[...], (1, 1))
    da = jnp.where(a_ref[...] > 0.0, dh, 0.0).astype(BF16)
    dw1[...] = dot(q_ref[...], da, (0, 0)).astype(BF16)
    pltpu.make_async_copy(dw1, dw1_hbm, sem.at[1]).start()
    lax.fori_loop(OUT_SLOTS, steps, step, 0)
    for i in range(steps - OUT_SLOTS, steps):
        out_copy(i, i % OUT_SLOTS).wait()
    pltpu.make_async_copy(loss_ref, loss_hbm, sem.at[0]).wait()
    pltpu.make_async_copy(dw1, dw1_hbm, sem.at[1]).wait()
    pltpu.make_async_copy(dw2, dw2_hbm, sem.at[2]).wait()


def solution(mesh):
    n = mesh.shape["tp"]

    def local_step(queries, w_first, w_second, catalogue, log_q, labels):
        own, d_in = queries.shape
        hid, emb = w_second.shape
        items = catalogue.shape[0]
        rows = own * n
        hbm = pl.BlockSpec(memory_space=pl.ANY)
        vmem = pl.BlockSpec(memory_space=pltpu.VMEM)
        dma = pltpu.SemaphoreType.DMA
        held = pl.pallas_call(
            functools.partial(loss_kernel, n),
            name="loss_kernel",
            out_shape=[
                pltpu.VMEM((rows, items), BF16),
                pltpu.VMEM((rows, emb), BF16),
                pltpu.VMEM((rows, emb), BF16),
                pltpu.VMEM((rows, hid), BF16),
                pltpu.VMEM((rows, hid), F32),
                pltpu.VMEM((rows, d_in), BF16),
                pltpu.VMEM((hid, emb), BF16),
                pltpu.VMEM((1, 1), F32),
            ],
            in_specs=[hbm] * 5 + [pl.BlockSpec(memory_space=pltpu.SMEM)],
            out_specs=[vmem] * 8,
            scratch_shapes=[
                pltpu.VMEM((items, emb), BF16),
                pltpu.VMEM((rows, items), F32),
                pltpu.VMEM((1, items), F32),
                pltpu.VMEM((d_in, hid), BF16),
                pltpu.VMEM((rows, LANES), jnp.int32),
                pltpu.VMEM((rows, LANES), jnp.int32),
                pltpu.VMEM((rows, LANES), F32),
                pltpu.VMEM((rows, LANES), F32),
                pltpu.VMEM((rows, LANES), F32),
                pltpu.VMEM((items // FIRST_TILE, rows, LANES), F32),
                pltpu.VMEM((n, 8, LANES), F32),
                pltpu.VMEM((rows, emb), F32),
                pltpu.VMEM((n, own, emb), F32),
                dma((4,)),
                dma((items // LOAD_TILE,)),
                dma((5, n - 1)),
                dma((n,)),
                dma((n,)),
                dma((n,)),
                dma((n,)),
                dma((n,)),
            ],
            compiler_params=pltpu.CompilerParams(collective_id=0, has_side_effects=True, vmem_limit_bytes=46 << 20),
        )(queries, w_first, w_second, catalogue, log_q.reshape(1, items), labels)
        loss, grad_items, grad_first, grad_second = pl.pallas_call(
            grad_kernel,
            name="grad_kernel",
            out_shape=[
                jax.ShapeDtypeStruct((1, 1), F32),
                jax.ShapeDtypeStruct((items, emb), BF16),
                jax.ShapeDtypeStruct((d_in, hid), BF16),
                jax.ShapeDtypeStruct((hid, emb), BF16),
            ],
            in_specs=[vmem] * 8,
            out_specs=[hbm] * 4,
            scratch_shapes=[
                pltpu.VMEM((OUT_SLOTS, OUT_TILE, emb), BF16),
                pltpu.VMEM((d_in, hid), BF16),
                pltpu.VMEM((hid, emb), BF16),
                dma((OUT_SLOTS,)),
                dma((3,)),
            ],
            compiler_params=pltpu.CompilerParams(vmem_limit_bytes=40 << 20),
        )(*held)
        return loss.reshape(1), grad_items, grad_first, grad_second

    row_spec = P(("dp", "tp"), None)
    return jax.shard_map(
        local_step, mesh=mesh,
        in_specs=(row_spec, P(None, None), P(None, None), P("tp", None), P("tp"), P(("dp", "tp"))),
        out_specs=(P("dp"), row_spec, P("dp", None), P("dp", None)), check_vma=False)
```

time: 202 us -> 52 us (0.26)
  blocking collectives: 112 us -> 0 us
  Pallas kernels: 0 us -> 51.3 us
  matrix products: 39.3 us -> 0 us
  other arithmetic: 17.4 us -> 0 us
  between operations: 16.6 us -> 0.64 us
  waiting for transfers between devices: 8.68 us -> 0 us
  local copies, waits for them, and re-layouts: 6.33 us -> 0 us
    psum x2 -> x0, blocking collectives: 67.9 us -> none  [the longest x1 55 us: local_step(): grad_first, grad_second = lax.psum((first_part, second_part), 'tp')]
    pallas_call x0 -> x2, Pallas kernels: none -> 51.3 us  [the longest x1 41.5 us: local_step(): pl.pallas_call(functools.partial(loss_kernel, n), name='loss_kernel', out...]
    dot_general x7 -> x0, matrix products: 39.3 us -> none  [the longest x1 14.1 us: local_step(): lax.dot_general(grad_logits, emb_all, (((0,), (0,)), ((), ())), preferred...]
    all_gather x1 -> x0, blocking collectives: 19 us -> none  [local_step(): emb_all = lax.all_gather(query_emb, 'tp', axis=0, tiled=True)]
    pmax x1 -> x0, blocking collectives: 14.1 us -> none  [local_step(): row_max = lax.pmax(local_max, 'tp')]
    unnamed x1 -> x0, blocking collectives: 11.1 us -> none
    reduce_scatter x1 -> x0, waiting for transfers between devices: 8.63 us -> none  [local_step(): lax.psum_scatter(emb_part, 'tp', scatter_dimension=0, tiled=True)]
    convert_element_type x1 -> x0, other arithmetic: 8.41 us -> none  [local_step(): (jnp.where(label_hit, soft_prob - 1.0, soft_prob) / total_rows).astype(jn...]
  transfers between devices with their start and end apart: 1 -> 0, of which waited for: 1 -> 0; matrix products, arithmetic and copies ran while one was open for 7% -> 0% of each run, Pallas kernels for 0% -> 0%
where the time goes in v1:
time: 52 us; the launch traced here: 51.9 us
  Pallas kernels  51.3 us (99%)
  between operations  0.64 us (1%)
    pallas_call x1, Pallas kernels, local_step(): pl.pallas_call(functools.partial(loss_kernel, n), name='loss_kernel', out...  41.5 us
    pallas_call x1, Pallas kernels, local_step(): pl.pallas_call(grad_kernel, name='grad_kernel', out_shape=[jax.ShapeDtype...  9.8 us

profile of v1, /device:TPU:113, one launch (start us, length us, event | category | flops | bytes accessed | tf_op | source)
XLA Modules:
  0.0 51.9 jit_solution(53452455585432819)
XLA Ops:
  0.6 41.5 %loss_kernel.1 = (bf16[128,32768]{1,0:T(8,128)(2,1)S(1)}, bf16[128,256]{1,0:T(8,128)(2,1)S(1)}, bf16[128,256]{1,0:T(8,128)(2,1)S(1)}, bf16[128,1024]{1,0:T(8,128...) custom-call(bf16[16,256]{1,0:T(8,128)(2,1)} %q_hbm.1, ...), custom_call_target="tpu_custom_call" | custom-call | tf_op jit(solution)/shard_map/loss_kernel/pallas_call | solution.py:217
  42.1 9.8 %grad_kernel.1 = (f32[1,1]{1,0:T(1,128)}, bf16[32768,256]{1,0:T(8,128)(2,1)}, bf16[256,1024]{1,0:T(8,128)(2,1)}, bf16[1024,256]{1,0:T(8,128)(2,1)}) custom-call(bf16[128,32768]{1,0:T(8,128)(2,1)S(1)} %get-tuple-element.16.g_ref, bf16[128,256]{1,0:T(8,128)(2,1)S(1)} %get-tuple-element.17.x_ref, bf16[128,256]{1,0:T(8,128)(2,1)S(1)} %get-tuple-element.18.dx_ref, ...), custom_call_target="tpu_custom_call" | custom-call | tf_op jit(solution)/shard_map/grad_kernel/pallas_call | solution.py:257
